TPU v7x, 16 devices: a whole 2x2x2 slice. The times are simulated.
16 devices in a mesh: dp: 4 (over z, y), tp: 4 (over x, core).
Axes of the slice: x: 2, y: 2, z: 2, core: 2. Of those that a mesh axis runs over, the one named last changes fastest.
Arguments:
- tokens: bfloat16 [8, 128, 5120], P('dp'), parts along dimension 0
- seq_lens: int32 [8], P('dp'), parts along dimension 0
- w_q: bfloat16 [5120, 5120], P(None, 'tp')
- w_k: bfloat16 [5120, 5120], P(None, 'tp')
- w_v: bfloat16 [5120, 5120], P(None, 'tp')
- w_o: bfloat16 [5120, 5120], P('tp')
- g_q: bfloat16 [5120], P('tp')
- g_k: bfloat16 [5120], P('tp')
- g_attn: bfloat16 [5120], replicated
- g_mlp: bfloat16 [5120], replicated
- w_gate: bfloat16 [5120, 13824], P(None, 'tp')
- w_up: bfloat16 [5120, 13824], P(None, 'tp')
- w_down: bfloat16 [13824, 5120], P('tp')
Outputs:
- output 1: bfloat16 [8, 128, 5120], P('dp'), parts along dimension 0
- output 2: bfloat16 [8, 40, 128, 128], P('dp', 'tp'), parts along dimension 0
- output 3: bfloat16 [8, 40, 128, 128], P('dp', 'tp'), parts along dimension 0
There are 4 independent parts. A program takes and returns all parts, laid end to end along the dimension named above; an argument that names none is the same for every part.
All inputs are finite; a program needn't handle non-finite values.
Results may differ from a plain program's by a relative error of at most 0.0163826.
Values are sent between devices in bfloat16 or wider.
A program may use at most 1 GiB of HBM per device.

v0:
```python
import jax
import jax.numpy as jnp
import numpy as np
from jax import lax
from jax.experimental import pallas as pl
from jax.experimental.pallas import tpu as pltpu
from jax.sharding import PartitionSpec as P

HEAD_DIM = 128
ROPE_BASE = 500000.0
NORM_EPS = 1e-6
F32 = jnp.float32
BF16 = jnp.bfloat16

WIDTH = 5120
RING = 6
KEEP = 12
N_V, N_QKV = 10, 15
N_G = 27
N_RG = N_G - KEEP
N_MLP = N_RG + 20


def rope_tables(seq_len):
    half = HEAD_DIM // 2
    inv_freq = (ROPE_BASE ** (-2.0 * np.arange(half) / HEAD_DIM)).astype(np.float32)
    angles = np.arange(seq_len, dtype=np.float32)[:, None] * inv_freq[None, :]
    cos, sin = np.cos(angles), np.sin(angles)
    return (np.concatenate([cos, cos], -1).astype(np.float32), np.concatenate([-sin, sin], -1).astype(np.float32))


def cols(start, size):
    return pl.ds(pl.multiple_of(start, size), size)


def dot(a, b):
    return jnp.dot(a, b, preferred_element_type=F32)


def layer_kernel(seq_ref, cos_hbm, sin_hbm, gq_hbm, gk_hbm, ga_hbm, gm_hbm,
                 x_hbm, wq, wk, wv, wo, wg, wu, wd,
                 yh_hbm, m_hbm, rs_hbm, kc_hbm, vc_hbm,
                 pool, x, qk, kb, vb, act, rsc, ssq_send, ssq_recv,
                 sends, rs_recv, xs_recv, other, rs_out,
                 gq16, gk16, ga16, gm16, gq_ref, gk_ref, ga_ref, gm_ref,
                 wsem, xsem, csem, ysem, ssq_s, ssq_r, arsem, tsem):
    t = lax.axis_index("tp")
    core = lax.rem(t, 2)
    sib = t + 1 - 2 * core
    xpeer = lax.rem(t + 2, 4)
    diag = 3 - t

    cos_ref, sin_ref = (rs_out.at[r, pl.ds(0, 128)] for r in range(2))

    def load(src, dst, slot):
        pltpu.make_async_copy(src, dst, wsem.at[slot]).start()

    def load_qk(n):
        slot = lax.rem(n, RING)

        @pl.when(lax.rem(n, 2) == 0)
        def _():
            load(wq.at[:, cols((n // 2) * 256, 256)], pool.at[slot], slot)

        @pl.when(lax.rem(n, 2) == 1)
        def _():
            load(wk.at[:, cols((n // 2) * 256, 256)], pool.at[slot], slot)

    def load_v(n):
        slot = lax.rem(n, RING)
        load(wv.at[:, cols((n - N_V) * 256, 256)], pool.at[slot], slot)

    def load_o(j):
        slot = RING + j
        for k in range(4):
            half = core if k // 2 else 1 - core
            load(wo.at[:, cols(half * 2560 + j * 512 + (k % 2) * 256, 256)], pool.at[slot, pl.ds(k * 1280, 1280), :], slot)

    def load_g(k, slot):
        @pl.when(jnp.logical_and(lax.rem(k, 2) == 0, k < N_G - 1))
        def _():
            load(wg.at[:, cols((k // 2) * 256, 256)], pool.at[slot], slot)

        @pl.when(lax.rem(k, 2) == 1)
        def _():
            load(wu.at[:, cols((k // 2) * 256, 256)], pool.at[slot], slot)

        @pl.when(k == N_G - 1)
        def _():
            load(wg.at[:, pl.ds(3328, 128)], pool.at[slot, :, pl.ds(0, 128)], slot)
            load(wu.at[:, pl.ds(3328, 128)], pool.at[slot, :, pl.ds(128, 128)], slot)

    def keep_slot(k):
        return RING + lax.rem(k + 5, KEEP)

    def ring_slot(b, l):
        return lax.rem(N_QKV + N_MLP * b + l, RING)

    def load_ring(b, l, lo, hi):
        slot = ring_slot(b, l)

        def g():
            load_g(KEEP + l, slot)

        def d():
            q = l - N_RG
            half = lax.rem(lax.rem(q, 4) // 2 + 1 + core, 2)
            load(wd.at[:, cols(half * 2560 + (q // 4) * 512 + lax.rem(q, 2) * 256, 256)], pool.at[slot, pl.ds(0, 3456), :], slot)

        def nxt():
            load_g(KEEP + l - N_MLP, slot)

        for start, end, fn in ((0, N_RG, g), (N_RG, N_MLP, d), (N_MLP, 2 * N_MLP, nxt if b == 0 else None)):
            if fn is None or hi < start or lo >= end:
                continue
            if lo >= start and hi < end:
                fn()
            else:
                pl.when(jnp.logical_and(l >= start, l < end))(fn)

    def wait_slot(slot, rows=WIDTH):
        src = wq if rows == WIDTH else wd
        pltpu.make_async_copy(src.at[:, pl.ds(0, 256)], pool.at[slot, pl.ds(0, rows), :], wsem.at[slot]).wait()

    def i32(v):
        return jnp.int32(v)

    xcopies = [pltpu.make_async_copy(x_hbm.at[pl.ds(b * 128, 128)], x.at[pl.ds(b * 128, 128)], xsem.at[b]) for b in range(2)]
    for c in xcopies:
        c.start()
    for n in range(2):
        load_qk(i32(n))
    small = [pltpu.make_async_copy(src, dst, tsem.at[i]) for i, (src, dst) in enumerate(
        ((cos_hbm, cos_ref), (sin_hbm, sin_ref), (gq_hbm, gq16), (gk_hbm, gk16), (ga_hbm, ga16), (gm_hbm, gm16)))]
    for c in small:
        c.start()

    barrier = pltpu.get_barrier_semaphore()
    for peer in (sib, xpeer, diag):
        pl.semaphore_signal(barrier, inc=1, device_id={"tp": peer}, device_id_type=pl.DeviceIdType.MESH)

    def remote(src, dst, ssem, rsem, peer):
        return pltpu.make_async_remote_copy(src_ref=src, dst_ref=dst, send_sem=ssem, recv_sem=rsem,
                                            device_id={"tp": peer}, device_id_type=pl.DeviceIdType.MESH)

    rsc[...] = jnp.zeros_like(rsc)
    for c in xcopies:
        c.wait()
    for n in range(2, 4):
        load_qk(i32(n))

    def qk_step(i, carry):
        n = 2 * i
        s0, s1 = lax.rem(n, RING), lax.rem(n + 1, RING)
        wait_slot(s0)
        wait_slot(s1)
        for m in (n + 4, n + 5):
            pl.when(m < N_V)(lambda m=m: load_qk(m))
            pl.when(m >= N_V)(lambda m=m: load_v(m))
        q = dot(x[...], pool[s0])
        k = dot(x[...], pool[s1])
        for b in range(2):
            for hh in range(2):
                qk[b, 2 * i + hh] = q[b * 128:(b + 1) * 128, hh * 128:(hh + 1) * 128]
                qk[b, 10 + 2 * i + hh] = k[b * 128:(b + 1) * 128, hh * 128:(hh + 1) * 128]
        rsc[0] += q[:, :128] * q[:, :128] + q[:, 128:] * q[:, 128:]
        rsc[1] += k[:, :128] * k[:, :128] + k[:, 128:] * k[:, 128:]
        return carry

    with jax.named_scope("qk"):
        lax.fori_loop(0, 5, qk_step, 0)
    load_v(i32(14))
    load_o(0)

    for r in range(2):
        ssq_send[r:r + 1, :] = jnp.sum(jnp.transpose(rsc[r]), axis=0, keepdims=True)
    ssq_send[2:8, :] = jnp.zeros((6, 256), F32)
    with jax.named_scope("barrier"):
        pl.semaphore_wait(barrier, 3)
    ssq_copies = [remote(ssq_send, ssq_recv.at[j], ssq_s.at[j], ssq_r.at[j], peer) for j, peer in enumerate((sib, xpeer, diag))]
    for c in ssq_copies:
        c.start()

    with jax.named_scope("v"):
        for group in ((10, 11), (12, 13, 14)):
            for n in group:
                wait_slot(n % RING)
            if group[0] == 10:
                load_o(1)
                load_o(2)
            else:
                load_o(3)
                load_o(4)
                for k in range(KEEP - 5):
                    load_g(i32(k), keep_slot(i32(k)))
            vals = [[dot(x[pl.ds(b * 128, 128), :], pool[n % RING]).astype(BF16) for b in range(2)] for n in group]
            for n, v in zip(group, vals):
                for b in range(2):
                    for hh in range(2):
                        vb[b, 2 * (n - N_V) + hh] = v[b][:, hh * 128:(hh + 1) * 128]
    vcopy = pltpu.make_async_copy(vb, vc_hbm, csem.at[0])
    vcopy.start()
    for l in range(RING):
        load_ring(0, i32(l), l, l)

    with jax.named_scope("ssqwait"):
        for c in ssq_copies:
            c.wait()
    for c in small:
        c.wait()
    for src, dst in ((gq16, gq_ref), (gk16, gk_ref), (ga16, ga_ref), (gm16, gm_ref)):
        dst[...] = src[...].astype(F32)
    total = ssq_send[...] + ssq_recv[0] + ssq_recv[1] + ssq_recv[2]
    scale = lax.rsqrt(total * (1.0 / WIDTH) + NORM_EPS)
    for r in range(2):
        rsc[r] = jnp.transpose(jnp.broadcast_to(scale[r:r + 1, :], (128, 256)))

    def rope(v):
        return (v * cos_ref[...] + pltpu.roll(v, 64, 1) * sin_ref[...]).astype(BF16)

    def qb(h):
        return act.at[:, pl.ds(h * 128, 128)]

    def attention(b):
        rows = pl.ds(b * 128, 128)
        row = lax.broadcasted_iota(jnp.int32, (128, 128), 0)
        col = lax.broadcasted_iota(jnp.int32, (128, 128), 1)
        allowed = jnp.logical_and(col <= row, col < seq_ref[b])
        for h in range(10):
            qb(h)[...] = rope(qk[b, h] * rsc[0, rows, :] * gq_ref[h:h + 1, :])
            kb[b, h] = rope(qk[b, 10 + h] * rsc[1, rows, :] * gk_ref[h:h + 1, :])
        for h in range(10):
            qk[b, h] = lax.dot_general(qb(h)[...], kb[b, h], (((1,), (1,)), ((), ())), preferred_element_type=F32)
        for h in range(10):
            s = jnp.where(allowed, qk[b, h] * HEAD_DIM ** -0.5, -1e30)
            e = jnp.exp(s - jnp.max(s, axis=-1, keepdims=True))
            qb(h)[...] = (e / jnp.sum(e, axis=-1, keepdims=True)).astype(BF16)
        for h in range(10):
            act[:, pl.ds(1280 + h * 128, 128)] = dot(qb(h)[...], vb[b, h]).astype(BF16)

    def rs_copy(p, b, j):
        return remote(sends.at[b, j], rs_recv.at[b, j], arsem.at[p, b, 0, j], arsem.at[p, b, 1, j], sib)

    def xs_copy(p, b, j):
        return remote(sends.at[b, j], xs_recv.at[p, b, j], arsem.at[p, b, 2, j], arsem.at[p, b, 3, j], xpeer)

    def ag_copy(p, b, j):
        return remote(xs_recv.at[p, b, j], other.at[b, j], arsem.at[p, b, 4, j], arsem.at[p, b, 5, j], sib)

    def send_sib(p, b, j, parts):
        for k in range(2):
            sends[b, j, :, pl.ds(k * 256, 256)] = parts[k].astype(BF16)
        rs_copy(p, b, j).start()

    def keep_own(j, parts):
        for k in range(4):
            qk[0, lax.rem(j, 3) * 4 + k] = parts[k // 2][:, (k % 2) * 128:(k % 2 + 1) * 128]

    def chip_sum(p, b, j):
        rs_copy(p, b, j).wait()
        for k in range(4):
            cs = pl.ds(k * 128, 128)
            sends[b, j, :, cs] = (qk[0, lax.rem(j, 3) * 4 + k] + rs_recv[b, j, :, cs].astype(F32)).astype(BF16)
        if (p, b) != (0, 1):
            xs_copy(p, b, j).start()

    def add_squares(half, b, v):
        v = v.astype(F32)
        rsc[half, pl.ds(b * 128, 128), :] += v[:, :128] * v[:, :128] + v[:, 128:256] * v[:, 128:256] + v[:, 256:384] * v[:, 256:384] + v[:, 384:] * v[:, 384:]

    def gather(p, b):
        for half in range(2):
            rsc[half, pl.ds(b * 128, 128), :] = jnp.zeros((128, 128), F32)

        def step(j, carry):
            with jax.named_scope(f"xwait{p}{b}"):
                xs_copy(p, b, j).wait()
            v = (sends[b, j].astype(F32) + xs_recv[p, b, j].astype(F32)).astype(BF16)
            xs_recv[p, b, j] = v
            ag_copy(p, b, j).start()
            add_squares(0, b, v)
            if (p, b) == (0, 0):
                @pl.when(j == 3)
                def _():
                    for c in range(5):
                        xs_copy(0, 1, c).start()
            return carry

        lax.fori_loop(0, 5, step, 0)

    def arrive(p, b):
        def step(j, carry):
            ag_copy(p, b, j).wait()
            add_squares(1, b, other[b, j])
            return carry

        lax.fori_loop(0, 5, step, 0)
        rs = lax.rsqrt(jnp.sum(rsc[0, pl.ds(b * 128, 128), :] + rsc[1, pl.ds(b * 128, 128), :], axis=-1, keepdims=True) * (1.0 / WIDTH) + NORM_EPS)
        rs_out[p, pl.ds(b * 128, 128), :] = jnp.broadcast_to(rs, (128, 128))

    def add_branch(p, b):
        rows = pl.ds(b * 128, 128)
        gain_ref = gm_ref if p else ga_ref

        def apply(j, carry):
            for half, ref in ((core, xs_recv.at[p]), (1 - core, other)):
                for w in range(4):
                    cs = cols(half * 2560 + j * 512 + w * 128, 128)
                    gain = gain_ref[pl.ds(half * 20 + j * 4 + w, 1), :]
                    x[rows, cs] = (x[rows, cs].astype(F32) + ref[b, j, :, pl.ds(w * 128, 128)].astype(F32) * rs_out[p, rows, :] * gain).astype(BF16)
            return carry

        lax.fori_loop(0, 5, apply, 0)

    yhcopies = [pltpu.make_async_copy(x.at[pl.ds(b * 128, 128)], yh_hbm.at[pl.ds(b * 128, 128)], ysem.at[b]) for b in range(2)]

    def project(b):
        def step(j, carry):
            slot = RING + j
            if b == 0:
                wait_slot(slot)
            parts = [dot(act[:, pl.ds(1280, 1280)], pool[slot, pl.ds(k * 1280, 1280), :]) for k in range(4)]
            send_sib(0, b, j, parts[:2])
            keep_own(j, parts[2:])
            pl.when(j > 1)(lambda: chip_sum(0, b, j - 2))
            return carry

        lax.fori_loop(0, 5, step, 0)
        chip_sum(0, b, i32(3))
        chip_sum(0, b, i32(4))

    for b in range(2):
        with jax.named_scope(f"attn{b}"):
            attention(b)
        with jax.named_scope(f"o{b}"):
            project(b)
    kcopy = pltpu.make_async_copy(kb, kc_hbm, csem.at[1])
    kcopy.start()
    for k in range(KEEP - 5, KEEP):
        load_g(i32(k), keep_slot(i32(k)))

    def gu_store(i, g, u):
        act[:, cols(i * 256, 256)] = (g * jax.nn.sigmoid(g) * u).astype(BF16)

    def gate_up(b):
        xb = x.at[pl.ds(b * 128, 128)]

        def ring_pair(l):
            s0, s1 = ring_slot(b, l), ring_slot(b, l + 1)
            wait_slot(s0)
            wait_slot(s1)
            return s0, s1

        def step(i, carry):
            l = 2 * i
            s0, s1 = ring_pair(l)
            k0, k1 = keep_slot(2 * i), keep_slot(2 * i + 1)
            if b == 0:
                wait_slot(k0)
                wait_slot(k1)
            gu_store(i + KEEP // 2, dot(xb[...], pool[s0]), dot(xb[...], pool[s1]))
            gu_store(i, dot(xb[...], pool[k0]), dot(xb[...], pool[k1]))
            load_ring(b, l + RING, RING, KEEP - 2 + RING)
            load_ring(b, l + 1 + RING, 1 + RING, KEEP - 1 + RING)
            return carry

        with jax.named_scope(f"gu{b}"):
            lax.fori_loop(0, KEEP // 2, step, 0)
            s0, s1 = ring_pair(i32(N_RG - 3))
            s2 = ring_slot(b, i32(N_RG - 1))
            wait_slot(s2)
            gu_store(i32(N_G // 2 - 1), dot(xb[...], pool[s0]), dot(xb[...], pool[s1]))
            r = dot(xb[...], pool[s2])
            g = r[:, :128]
            act[:, 3328:3456] = (g * jax.nn.sigmoid(g) * r[:, 128:]).astype(BF16)
            for l in range(N_RG - 3, N_RG):
                load_ring(b, i32(l + RING), l + RING, l + RING)

    def down(b):
        def blocks(first):
            slots = [ring_slot(b, first + k) for k in range(2)]
            for sl in slots:
                wait_slot(sl, 3456)
            return [dot(act[...], pool[sl, pl.ds(0, 3456), :]) for sl in slots]

        def refill(first):
            for k in range(2):
                l = first + k + RING
                if b == 0:
                    load_ring(b, l, N_RG + RING, N_MLP - 1 + RING)
                else:
                    pl.when(l < N_MLP)(lambda l=l: load_ring(b, l, N_RG + RING, N_MLP - 1))

        def step(j, carry):
            l = N_RG + 4 * j
            send_sib(1, b, j, blocks(l))
            refill(l)
            keep_own(j, blocks(l + 2))
            refill(l + 2)
            chip_sum(1, b, j)
            return carry

        with jax.named_scope(f"d{b}"):
            lax.fori_loop(0, 5, step, 0)

    with jax.named_scope("gather00"):
        gather(0, 0)
    with jax.named_scope("norm00"):
        arrive(0, 0)
        add_branch(0, 0)
    gate_up(0)
    with jax.named_scope("gather01"):
        gather(0, 1)
    down(0)
    with jax.named_scope("norm01"):
        arrive(0, 1)
        add_branch(0, 1)
        yhcopies[1].start()
    gate_up(1)
    with jax.named_scope("gather10"):
        gather(1, 0)
    down(1)
    with jax.named_scope("arrive10"):
        arrive(1, 0)
        add_branch(1, 0)
        yhcopies[0].start()
    with jax.named_scope("gather11"):
        gather(1, 1)
    mcopies = [pltpu.make_async_copy(ref, m_hbm.at[pl.ds(half * 5, 5)], ysem.at[3 + i]) for i, (half, ref) in enumerate(((core, xs_recv.at[1, 1]), (1 - core, other.at[1])))]
    mcopies[0].start()
    with jax.named_scope("arrive11"):
        arrive(1, 1)
    mcopies[1].start()
    rcopy = pltpu.make_async_copy(rs_out.at[1, pl.ds(128, 128)], rs_hbm, ysem.at[2])
    rcopy.start()
    with jax.named_scope("tail"):
        for c in [vcopy, kcopy, rcopy] + yhcopies + mcopies:
            c.wait()


def finish_kernel(rs_hbm, gm_hbm, yh_hbm, m_hbm, k_in, v_in, y_hbm, k_out, v_out, rs, gm, yh, m, kb, vb, isem, msem, hsem, psem, osem, ysem):
    def chunk(c):
        cs = pl.ds(c * 512, 512)
        return [pltpu.make_async_copy(m_hbm.at[c], m.at[c], msem.at[c]), pltpu.make_async_copy(yh_hbm.at[pl.ds(128, 128), cs], yh.at[pl.ds(128, 128), cs], hsem.at[c])]

    top = pl.ds(0, 128)
    moves = ((yh_hbm.at[top], yh.at[top], y_hbm.at[top]), (k_in, kb, k_out), (v_in, vb, v_out))
    loads = [pltpu.make_async_copy(src, buf, psem.at[i]) for i, (src, buf, dst) in enumerate(moves)]
    out = [pltpu.make_async_copy(buf, dst, osem.at[i]) for i, (src, buf, dst) in enumerate(moves)]
    for d in loads:
        d.start()
    small = [pltpu.make_async_copy(src, dst, isem.at[i]) for i, (src, dst) in enumerate(((rs_hbm, rs), (gm_hbm, gm)))]
    for d in small:
        d.start()
    for c in range(10):
        for d in chunk(c):
            d.start()
    for i in range(3):
        loads[i].wait()
        out[i].start()
    for d in small:
        d.wait()
    for c in range(10):
        for d in chunk(c):
            d.wait()
        for w in range(4):
            rows, cs = pl.ds(128, 128), pl.ds(c * 512 + w * 128, 128)
            g = gm[c * 4 + w:c * 4 + w + 1, :].astype(F32)
            yh[rows, cs] = (yh[rows, cs].astype(F32) + m[c, :, pl.ds(w * 128, 128)].astype(F32) * rs[...] * g).astype(BF16)
        rows, cs = pl.ds(128, 128), pl.ds(c * 512, 512)
        ycopy = pltpu.make_async_copy(yh.at[rows, cs], y_hbm.at[rows, cs], ysem.at[c])
        ycopy.start()
        out.append(ycopy)
    for d in out:
        d.wait()


def solution(mesh):
    def local_layer(tokens, seq_lens, w_q, w_k, w_v, w_o, g_q, g_k, g_attn, g_mlp, w_gate, w_up, w_down):
        cos_tab, sin_tab = rope_tables(128)
        hbm = pl.BlockSpec(memory_space=pl.ANY)
        gain = lambda g: g.reshape(-1, 128)
        dma = pltpu.SemaphoreType.DMA
        cache = jax.ShapeDtypeStruct((2, 10, 128, 128), BF16)
        hidden = jax.ShapeDtypeStruct((256, 5120), BF16)
        yh, m, rs, kc, vc = pl.pallas_call(
            layer_kernel,
            out_shape=(hidden, jax.ShapeDtypeStruct((10, 128, 512), BF16), jax.ShapeDtypeStruct((128, 128), F32), cache, cache),
            in_specs=[pl.BlockSpec(memory_space=pltpu.SMEM)] + [hbm] * 14,
            out_specs=(hbm,) * 5,
            scratch_shapes=[
                pltpu.VMEM((RING + KEEP, 5120, 256), BF16),
                pltpu.VMEM((256, 5120), BF16),
                pltpu.VMEM((2, 20, 128, 128), F32),
                pltpu.VMEM((2, 10, 128, 128), BF16),
                pltpu.VMEM((2, 10, 128, 128), BF16),
                pltpu.VMEM((128, 3456), BF16),
                pltpu.VMEM((2, 256, 128), F32),
                pltpu.VMEM((8, 256), F32),
                pltpu.VMEM((3, 8, 256), F32),
                pltpu.VMEM((2, 5, 128, 512), BF16),
                pltpu.VMEM((2, 5, 128, 512), BF16),
                pltpu.VMEM((2, 2, 5, 128, 512), BF16),
                pltpu.VMEM((2, 5, 128, 512), BF16),
                pltpu.VMEM((2, 256, 128), F32),
                pltpu.VMEM((10, 128), BF16),
                pltpu.VMEM((10, 128), BF16),
                pltpu.VMEM((40, 128), BF16),
                pltpu.VMEM((40, 128), BF16),
                pltpu.VMEM((10, 128), F32),
                pltpu.VMEM((10, 128), F32),
                pltpu.VMEM((40, 128), F32),
                pltpu.VMEM((40, 128), F32),
                dma((RING + KEEP,)), dma((2,)), dma((2,)), dma((6,)), dma((3,)), dma((3,)), dma((2, 2, 6, 5)), dma((6,)),
            ],
            compiler_params=pltpu.CompilerParams(collective_id=0, has_side_effects=True, vmem_limit_bytes=67043328),
        )(seq_lens, jnp.asarray(cos_tab), jnp.asarray(sin_tab), gain(g_q), gain(g_k), gain(g_attn), gain(g_mlp),
          tokens.reshape(256, 5120), w_q, w_k, w_v, w_o, w_gate, w_up, w_down)
        y, kc, vc = pl.pallas_call(
            finish_kernel,
            out_shape=(hidden, cache, cache),
            in_specs=[hbm] * 6,
            out_specs=(hbm,) * 3,
            scratch_shapes=[
                pltpu.VMEM((128, 128), F32),
                pltpu.VMEM((40, 128), BF16),
                pltpu.VMEM((256, 5120), BF16),
                pltpu.VMEM((10, 128, 512), BF16),
                pltpu.VMEM((2, 10, 128, 128), BF16),
                pltpu.VMEM((2, 10, 128, 128), BF16),
                dma((2,)), dma((10,)), dma((10,)), dma((3,)), dma((3,)), dma((10,)),
            ],
            compiler_params=pltpu.CompilerParams(vmem_limit_bytes=60000000),
        )(rs, gain(g_mlp), yh, m, kc, vc)
        return y.reshape(2, 128, 5120), kc, vc

    return jax.shard_map(local_layer, mesh=mesh, in_specs=(P('dp', None, None), P('dp'), P(None, 'tp'), P(None, 'tp'), P(None, 'tp'), P('tp', None), P('tp'), P('tp'), P(), P(), P(None, 'tp'), P(None, 'tp'), P('tp', None)), out_specs=(P('dp', None, None), P('dp', 'tp', None, None), P('dp', 'tp', None, None)), check_vma=False)
```

profile of v0, /device:TPU:0, one launch (start us, length us, event | category | flops | bytes accessed | tf_op | source)
XLA Modules:
  0.0 99.8 jit_solution(9175931863866856349)
XLA Ops:
  0.6 94.5 %shard_map.166 = (bf16[256,5120]{1,0:T(8,128)(2,1)}, bf16[10,128,512]{2,1,0:T(8,128)(2,1)}, f32[128,128]{1,0:T(8,128)}, bf16[2,10,128,128]{3,2,1,0:T(8,128)(2,1)}, bf16[2,10,128,128]{3,2,1,0:T(8,128)(2,1)}) custom-call(s32[2]{0:T(128)} %seq_ref.1, f32[128,128]{1,0:T(8,128)} %constant.4.clone.cos_hbm, f32[128,128]{1,0:T(8,128)} %constant.5.clone.sin_hbm, ...), custom_call_target="tpu_custom_call" | custom-call | tf_op jit(solution)/shard_map/pallas_call | solution.py:486
  95.1 4.5 %shard_map.167 = (bf16[256,5120]{1,0:T(8,128)(2,1)}, bf16[2,10,128,128]{3,2,1,0:T(8,128)(2,1)}, bf16[2,10,128,128]{3,2,1,0:T(8,128)(2,1)}) custom-call(f32[128,128]{1,0:T(8,128)} %get-tuple-element.11.rs_hbm, bf16[40,128]{1,0:T(8,128)(2,1)} %bitcast.8, bf16[256,5120]{1,0:T(8,128)(2,1)} %get-tuple-element.12.yh_hbm, ...), custom_call_target="tpu_custom_call" | custom-call | tf_op jit(solution)/shard_map/pallas_call | solution.py:519
where the time goes:
time: 99.9 us; the launch traced here: 99.8 us
  Pallas kernels  99 us (99%)
    pallas_call x1, Pallas kernels, local_layer(): pl.pallas_call(layer_kernel, out_shape=(hidden, jax.ShapeDtypeStruct((10,...  94.5 us
    pallas_call x1, Pallas kernels, local_layer(): pl.pallas_call(finish_kernel, out_shape=(hidden, cache, cache), in_specs=...  4.46 us

commit v1 on v0

--- a/solution.py
+++ b/solution.py
@@ -319,15 +319,21 @@
             slot = RING + j
             if b == 0:
                 wait_slot(slot)
-            parts = [dot(act[:, pl.ds(1280, 1280)], pool[slot, pl.ds(k * 1280, 1280), :]) for k in range(4)]
-            send_sib(0, b, j, parts[:2])
-            keep_own(j, parts[2:])
-            pl.when(j > 1)(lambda: chip_sum(0, b, j - 2))
+            def blocks(first):
+                return [dot(act[:, pl.ds(1280, 1280)], pool[slot, pl.ds(k * 1280, 1280), :]) for k in (first, first + 1)]
+
+            send_sib(0, b, j, blocks(0))
+            keep_own(j, blocks(2))
+            if b == 0:
+                chip_sum(0, b, j)
+            else:
+                pl.when(j > 1)(lambda: chip_sum(0, b, j - 2))
             return carry
 
         lax.fori_loop(0, 5, step, 0)
-        chip_sum(0, b, i32(3))
-        chip_sum(0, b, i32(4))
+        if b == 1:
+            chip_sum(0, b, i32(3))
+            chip_sum(0, b, i32(4))
 
     for b in range(2):
         with jax.named_scope(f"attn{b}"):
@@ -397,11 +403,16 @@
             refill(l)
             keep_own(j, blocks(l + 2))
             refill(l + 2)
-            chip_sum(1, b, j)
+            if b == 1:
+                chip_sum(1, b, j)
+            else:
+                pl.when(j > 0)(lambda: chip_sum(1, b, j - 1))
             return carry
 
         with jax.named_scope(f"d{b}"):
             lax.fori_loop(0, 5, step, 0)
+            if b == 0:
+                chip_sum(1, b, i32(4))
 
     with jax.named_scope("gather00"):
         gather(0, 0)

time: 99.9 us -> 100 us (level)
  no operation moved by 1% of the time
where the time goes in v1:
time: 100 us
  Pallas kernels  99.2 us (99%)
    pallas_call x1, Pallas kernels, local_layer(): pl.pallas_call(layer_kernel, out_shape=(hidden, jax.ShapeDtypeStruct((10,...  94.7 us
    pallas_call x1, Pallas kernels, local_layer(): pl.pallas_call(finish_kernel, out_shape=(hidden, cache, cache), in_specs=...  4.46 us

profile of v1, /device:TPU:0, one launch (start us, length us, event | category | flops | bytes accessed | tf_op | source)
XLA Modules:
  0.0 100.0 jit_solution(13706766836527082549)
XLA Ops:
  0.6 94.7 %shard_map.166 = (bf16[256,5120]{1,0:T(8,128)(2,1)}, bf16[10,128,512]{2,1,0:T(8,128)(2,1)}, f32[128,128]{1,0:T(8,128)}, bf16[2,10,128,128]{3,2,1,0:T(8,128)(2,1)}, bf16[2,10,128,128]{3,2,1,0:T(8,128)(2,1)}) custom-call(s32[2]{0:T(128)} %seq_ref.1, f32[128,128]{1,0:T(8,128)} %constant.4.clone.cos_hbm, f32[128,128]{1,0:T(8,128)} %constant.5.clone.sin_hbm, ...), custom_call_target="tpu_custom_call" | custom-call | tf_op jit(solution)/shard_map/pallas_call | solution.py:497
  95.4 4.5 %shard_map.167 = (bf16[256,5120]{1,0:T(8,128)(2,1)}, bf16[2,10,128,128]{3,2,1,0:T(8,128)(2,1)}, bf16[2,10,128,128]{3,2,1,0:T(8,128)(2,1)}) custom-call(f32[128,128]{1,0:T(8,128)} %get-tuple-element.11.rs_hbm, bf16[40,128]{1,0:T(8,128)(2,1)} %bitcast.8, bf16[256,5120]{1,0:T(8,128)(2,1)} %get-tuple-element.12.yh_hbm, ...), custom_call_target="tpu_custom_call" | custom-call | tf_op jit(solution)/shard_map/pallas_call | solution.py:530

commit v2 on v1

--- a/solution.py
+++ b/solution.py
@@ -182,15 +182,16 @@
         c.start()
 
     with jax.named_scope("v"):
-        for group in ((10, 11), (12, 13, 14)):
+        for group in ((10, 11), (12, 13), (14,)):
             for n in group:
                 wait_slot(n % RING)
             if group[0] == 10:
                 load_o(1)
                 load_o(2)
-            else:
+            elif group[0] == 12:
                 load_o(3)
                 load_o(4)
+            else:
                 for k in range(KEEP - 5):
                     load_g(i32(k), keep_slot(i32(k)))
             vals = [[dot(x[pl.ds(b * 128, 128), :], pool[n % RING]).astype(BF16) for b in range(2)] for n in group]
@@ -403,16 +404,11 @@
             refill(l)
             keep_own(j, blocks(l + 2))
             refill(l + 2)
-            if b == 1:
-                chip_sum(1, b, j)
-            else:
-                pl.when(j > 0)(lambda: chip_sum(1, b, j - 1))
+            chip_sum(1, b, j)
             return carry
 
         with jax.named_scope(f"d{b}"):
             lax.fori_loop(0, 5, step, 0)
-            if b == 0:
-                chip_sum(1, b, i32(4))
 
     with jax.named_scope("gather00"):
         gather(0, 0)

time: 100 us -> 99.8 us (level)
  no operation moved by 1% of the time
where the time goes in v2:
time: 99.8 us; the launch traced here: 99.7 us
  Pallas kernels  98.9 us (99%)
    pallas_call x1, Pallas kernels, local_layer(): pl.pallas_call(layer_kernel, out_shape=(hidden, jax.ShapeDtypeStruct((10,...  94.4 us
    pallas_call x1, Pallas kernels, local_layer(): pl.pallas_call(finish_kernel, out_shape=(hidden, cache, cache), in_specs=...  4.46 us

profile of v2, /device:TPU:0, one launch (start us, length us, event | category | flops | bytes accessed | tf_op | source)
XLA Modules:
  0.0 99.7 jit_solution(6668631384289896378)
XLA Ops:
  0.6 94.4 %shard_map.166 = (bf16[256,5120]{1,0:T(8,128)(2,1)}, bf16[10,128,512]{2,1,0:T(8,128)(2,1)}, f32[128,128]{1,0:T(8,128)}, bf16[2,10,128,128]{3,2,1,0:T(8,128)(2,1)}, bf16[2,10,128,128]{3,2,1,0:T(8,128)(2,1)}) custom-call(s32[2]{0:T(128)} %seq_ref.1, f32[128,128]{1,0:T(8,128)} %constant.4.clone.cos_hbm, f32[128,128]{1,0:T(8,128)} %constant.5.clone.sin_hbm, ...), custom_call_target="tpu_custom_call" | custom-call | tf_op jit(solution)/shard_map/pallas_call | solution.py:493
  95.0 4.5 %shard_map.167 = (bf16[256,5120]{1,0:T(8,128)(2,1)}, bf16[2,10,128,128]{3,2,1,0:T(8,128)(2,1)}, bf16[2,10,128,128]{3,2,1,0:T(8,128)(2,1)}) custom-call(f32[128,128]{1,0:T(8,128)} %get-tuple-element.11.rs_hbm, bf16[40,128]{1,0:T(8,128)(2,1)} %bitcast.8, bf16[256,5120]{1,0:T(8,128)(2,1)} %get-tuple-element.12.yh_hbm, ...), custom_call_target="tpu_custom_call" | custom-call | tf_op jit(solution)/shard_map/pallas_call | solution.py:526
